TPU v7x, 32 devices: a whole 2x2x4 slice. The times are simulated.
32 devices in a mesh: dp: 2 (over x), tp: 4 (over z), sq: 4 (over y, core).
Axes of the slice: x: 2, y: 2, z: 4, core: 2. Of those that a mesh axis runs over, the one named last changes fastest.
Arguments:
- x_steps: bfloat16 [4, 32, 6144], P(None, 'dp'), parts along dimension 1
- positions: int32 [32], P('dp'), parts along dimension 0
- k_cache: bfloat16 [32, 4096, 4, 128], P('dp', 'sq', 'tp'), parts along dimension 0
- v_cache: bfloat16 [32, 4096, 4, 128], P('dp', 'sq', 'tp'), parts along dimension 0
- w_q: bfloat16 [6144, 6144], P(None, 'tp')
- b_q: bfloat16 [6144], P('tp')
- w_k: bfloat16 [6144, 512], P(None, 'tp')
- b_k: bfloat16 [512], P('tp')
- w_v: bfloat16 [6144, 512], P(None, 'tp')
- b_v: bfloat16 [512], P('tp')
- w_o: bfloat16 [6144, 6144], P('tp')
- b_o: bfloat16 [6144], replicated
- ln1_gain: bfloat16 [6144], replicated
- ln1_bias: bfloat16 [6144], replicated
- ln2_gain: bfloat16 [6144], replicated
- ln2_bias: bfloat16 [6144], replicated
- w_fc: bfloat16 [6144, 24576], P(None, 'tp')
- b_fc: bfloat16 [24576], P('tp')
- w_proj: bfloat16 [24576, 6144], P('tp')
- b_proj: bfloat16 [6144], replicated
Outputs:
- output 1: bfloat16 [4, 32, 6144], P(None, 'dp'), parts along dimension 1
- output 2: bfloat16 [32, 4096, 4, 128], P('dp', 'sq', 'tp'), parts along dimension 0
- output 3: bfloat16 [32, 4096, 4, 128], P('dp', 'sq', 'tp'), parts along dimension 0
There are 2 independent parts. A program takes and returns all parts, laid end to end along the dimension named above; an argument that names none is the same for every part.
All inputs are finite; a program needn't handle non-finite values.
Results may differ from a plain program's by a relative error of at most 0.015911.
Values sent between devices are 32-bit elements.
A program may use at most 1 GiB of HBM per device.

v0:
```python
import jax
import jax.numpy as jnp
from jax import lax
from jax.sharding import PartitionSpec as P

ROPE_BASE = 1000000.0
LN_EPS = 1e-5
NEG_BIG = -1e30


def layer_norm(vectors, gain, shift):
    row_mean = jnp.mean(vectors, axis=-1, keepdims=True)
    centered = vectors - row_mean
    row_var = jnp.mean(centered * centered, axis=-1, keepdims=True)
    return centered * lax.rsqrt(row_var + LN_EPS) * gain.astype(jnp.float32) + shift.astype(jnp.float32)


def rope_tables(positions, head_dim):
    half_dim = head_dim // 2
    inv_freq = jnp.power(jnp.float32(ROPE_BASE), -2.0 * jnp.arange(half_dim, dtype=jnp.float32) / head_dim)
    angle = positions.astype(jnp.float32)[..., None] * inv_freq
    return jnp.cos(angle), jnp.sin(angle)


def apply_rope(vectors, cos_t, sin_t):
    half_dim = vectors.shape[-1] // 2
    first = vectors[..., :half_dim]
    second = vectors[..., half_dim:]
    return jnp.concatenate([first * cos_t - second * sin_t, second * cos_t + first * sin_t], axis=-1)


def linear(rows_in, weight, bias):
    return jnp.dot(rows_in, weight, preferred_element_type=jnp.float32) + bias.astype(jnp.float32)


def new_entries(x_in, cur_pos, ln1_gain, ln1_bias, w_q, b_q, w_k, b_k, w_v, b_v, kv_count, head_dim):
    batch = x_in.shape[0]
    group = w_q.shape[1] // (kv_count * head_dim)
    hidden = layer_norm(x_in.astype(jnp.float32), ln1_gain, ln1_bias).astype(jnp.bfloat16)
    query = linear(hidden, w_q, b_q).astype(jnp.bfloat16)
    key_new = linear(hidden, w_k, b_k).astype(jnp.bfloat16)
    val_new = linear(hidden, w_v, b_v).astype(jnp.bfloat16)
    cos_t, sin_t = rope_tables(cur_pos, head_dim)
    q_rot = apply_rope(query.reshape(batch, kv_count, group, head_dim).astype(jnp.float32), cos_t[:, None, None, :], sin_t[:, None, None, :]).astype(jnp.bfloat16)
    k_rot = apply_rope(key_new.reshape(batch, kv_count, head_dim).astype(jnp.float32), cos_t[:, None, :], sin_t[:, None, :]).astype(jnp.bfloat16)
    return q_rot, k_rot, val_new.reshape(batch, kv_count, head_dim)


def partial_attention(q_rot, key_buf, val_buf, slot_ok, head_dim):
    slot_mask = slot_ok[:, None, None, :]
    scores = jnp.einsum("bgrd,bwgd->bgrw", q_rot, key_buf, preferred_element_type=jnp.float32) * head_dim ** -0.5
    scores = jnp.where(slot_mask, scores, NEG_BIG)
    part_max = jnp.max(scores, axis=-1)
    weights = jnp.where(slot_mask, jnp.exp(scores - part_max[..., None]), 0.0)
    part_sum = jnp.sum(weights, axis=-1)
    part_out = jnp.einsum("bgrw,bwgd->bgrd", weights.astype(jnp.bfloat16), val_buf, preferred_element_type=jnp.float32)
    return part_max, part_sum, part_out


def layer_tail(x_in, attn_out, w_o, b_o, ln2_gain, ln2_bias, w_fc, b_fc, w_proj, b_proj):
    attn_proj = lax.psum(jnp.dot(attn_out, w_o, preferred_element_type=jnp.float32), "tp")
    x_mid = (x_in.astype(jnp.float32) + attn_proj + b_o.astype(jnp.float32)).astype(jnp.bfloat16)
    hidden = layer_norm(x_mid.astype(jnp.float32), ln2_gain, ln2_bias).astype(jnp.bfloat16)
    gelu_out = jax.nn.gelu(linear(hidden, w_fc, b_fc), approximate=True).astype(jnp.bfloat16)
    mlp_out = lax.psum(jnp.dot(gelu_out, w_proj, preferred_element_type=jnp.float32), "tp")
    return (x_mid.astype(jnp.float32) + mlp_out + b_proj.astype(jnp.float32)).astype(jnp.bfloat16)


def solution(mesh):
    sq_size = mesh.shape["sq"]
    act_spec = P(None, "dp", None)
    cache_spec = P("dp", "sq", "tp", None)
    col_spec = P(None, "tp")
    row_spec = P("tp", None)
    vec_spec = P("tp")
    rep_spec = P(None)
    in_specs = (act_spec, P("dp"), cache_spec, cache_spec, col_spec, vec_spec, col_spec, vec_spec,
                col_spec, vec_spec, row_spec, rep_spec, rep_spec, rep_spec, rep_spec, rep_spec,
                col_spec, vec_spec, row_spec, rep_spec)
    out_specs = (act_spec, cache_spec, cache_spec)

    def per_device(x_steps, positions, key_buf, val_buf, w_q, b_q, w_k, b_k, w_v, b_v, w_o, b_o,
                   ln1_gain, ln1_bias, ln2_gain, ln2_bias, w_fc, b_fc, w_proj, b_proj):
        steps, batch = x_steps.shape[0], x_steps.shape[1]
        slots_local, kv_local, head_dim = key_buf.shape[1], key_buf.shape[2], key_buf.shape[3]
        slots = slots_local * sq_size
        first_slot = lax.axis_index("sq") * slots_local
        slot_ids = first_slot + jnp.arange(slots_local, dtype=jnp.int32)
        batch_ids = jnp.arange(batch, dtype=jnp.int32)
        outputs = []
        for step_idx in range(steps):
            x_in = x_steps[step_idx]
            cur_pos = positions + step_idx
            q_rot, k_rot, v_heads = new_entries(x_in, cur_pos, ln1_gain, ln1_bias, w_q, b_q, w_k, b_k, w_v, b_v, kv_local, head_dim)
            local_slot = cur_pos % slots - first_slot
            local_slot = jnp.where((local_slot >= 0) & (local_slot < slots_local), local_slot, slots_local)
            key_buf = key_buf.at[batch_ids, local_slot].set(k_rot, mode="drop")
            val_buf = val_buf.at[batch_ids, local_slot].set(v_heads, mode="drop")
            held_pos = cur_pos[:, None] - (cur_pos[:, None] - slot_ids[None, :]) % slots
            part_max, part_sum, part_out = partial_attention(q_rot, key_buf, val_buf, held_pos >= 0, head_dim)
            stats = jnp.concatenate([part_out, part_sum[..., None], part_max[..., None]], axis=-1)
            gathered = lax.all_gather(stats, "sq")
            all_max = gathered[..., head_dim + 1]
            glob_max = jnp.max(all_max, axis=0)
            rescale = jnp.exp(all_max - glob_max)
            total_sum = jnp.sum(rescale * gathered[..., head_dim], axis=0)
            total_out = jnp.sum(rescale[..., None] * gathered[..., :head_dim], axis=0)
            attn_out = (total_out / total_sum[..., None]).astype(jnp.bfloat16).reshape(batch, -1)
            outputs.append(layer_tail(x_in, attn_out, w_o, b_o, ln2_gain, ln2_bias, w_fc, b_fc, w_proj, b_proj))
        return jnp.stack(outputs), key_buf, val_buf

    return jax.shard_map(per_device, mesh=mesh, in_specs=in_specs, out_specs=out_specs, check_vma=False)
```

profile of v0, /device:TPU:0, one launch (start us, length us, event | category | flops | bytes accessed | tf_op | source)
XLA Modules:
  0.0 529.3 jit_solution(15935317720218659532)
XLA Ops:
  7.2 4.8 copy.165
  12.0 2.0 copy.166
  14.4 0.4 fusion.92
  15.7 7.9 %fusion.1 = f32[16,1536]{1,0:T(8,128)S(1)} fusion(bf16[6144,1536]{1,0:T(8,128)(2,1)} %param.24, f32[1536]{0:T(1024)S(1)} %convert_element_type.401, f32[6144]{0:T(1024)S(1)} %convert_element_type.399, f32[6144]{0:T(1024)S(1)} %convert_element_type.398, f32[16]{0:T(128)S(1)} %add_rsqrt_fusion.7, f32[16]{0:T(128)S(1)} %get-tuple-element.109, ...), kind=kOutput, calls=%fused_computation.17 | convolution fusion | flops 302653440 | bytes 19227648 | tf_op jit(solution)/shard_map/dot_general | solution.py:33
  23.7 9.0 %fusion.3 = f32[16,1536]{1,0:T(8,128)S(1)} fusion(bf16[6144,1536]{1,0:T(8,128)(2,1)} %param.24, f32[1536]{0:T(1024)S(1)} %convert_element_type.401, f32[16]{0:T(128)S(1)} %add_rsqrt_fusion.5, f32[16]{0:T(128)S(1)} %get-tuple-element.108, f32[6144]{0:T(1024)S(1)} %convert_element_type.399, f32[6144]{0:T(1024)S(1)} %convert_element_type.398, ...), kind=kOutput, calls=%fused_computation.19 | convolution fusion | flops 302653440 | bytes 19227648 | tf_op jit(solution)/shard_map/dot_general | solution.py:33
  33.9 2.6 fusion.5
  37.2 2.6 fusion.7
  40.5 2.5 scatter_fusion
  43.0 2.5 scatter_fusion.1
  46.0 3.8 fusion.383
  50.2 0.8 convolution_bitcast_fusion.3
  51.7 20.7 %all-gather = f32[64,1,12,130]{3,1,2,0:T(1,128)S(1)} all-gather(f32[16,1,12,130]{3,1,2,0:T(1,128)S(1)} %copy.109), channel_id=2, replica_groups=mesh['dp'=2,'tp'=4,'sq'=4] {'sq'}, dimensions={0}, use_global_device_ids=true | all-gather | bytes 499200 | tf_op jit(solution)/shard_map/all_gather | solution.py:102
  72.8 0.6 slice_reduce_fusion.10
  73.9 2.5 scatter_fusion.2
  76.4 2.5 scatter_fusion.3
  79.0 3.7 fusion.382
  83.1 0.8 convolution_bitcast_fusion.2
  84.6 8.5 %all-gather.1 = f32[64,1,12,130]{3,1,2,0:T(1,128)S(1)} all-gather(f32[16,1,12,130]{3,1,2,0:T(1,128)S(1)} %copy.114), channel_id=3, replica_groups=mesh['dp'=2,'tp'=4,'sq'=4] {'sq'}, dimensions={0}, use_global_device_ids=true | all-gather | bytes 499200 | tf_op jit(solution)/shard_map/all_gather | solution.py:102
  93.5 0.6 slice_reduce_fusion.8
  94.4 2.5 scatter_fusion.4
  96.9 2.5 scatter_fusion.5
  99.5 3.7 fusion.381
  103.6 0.8 convolution_bitcast_fusion.1
  105.1 8.5 %all-gather.2 = f32[64,1,12,130]{3,1,2,0:T(1,128)S(1)} all-gather(f32[16,1,12,130]{3,1,2,0:T(1,128)S(1)} %copy.119), channel_id=4, replica_groups=mesh['dp'=2,'tp'=4,'sq'=4] {'sq'}, dimensions={0}, use_global_device_ids=true | all-gather | bytes 499200 | tf_op jit(solution)/shard_map/all_gather | solution.py:102
  114.0 0.6 slice_reduce_fusion.6
  114.9 2.5 scatter_fusion.6
  117.4 2.5 scatter_fusion.7
  120.0 3.7 fusion.380
  124.1 0.8 convolution_bitcast_fusion
  125.6 8.9 %all-gather.3 = f32[64,1,12,130]{3,1,2,0:T(1,128)S(1)} all-gather(f32[16,1,12,130]{3,1,2,0:T(1,128)S(1)} %copy.124), channel_id=5, replica_groups=mesh['dp'=2,'tp'=4,'sq'=4] {'sq'}, dimensions={0}, use_global_device_ids=true | all-gather | bytes 499200 | tf_op jit(solution)/shard_map/all_gather | solution.py:102
  134.9 0.6 slice_reduce_fusion.4
  135.8 9.9 %fusion.269 = f32[16,6144]{1,0:T(8,128)} fusion(bf16[1536,6144]{1,0:T(8,128)(2,1)} %param.30, f32[16,12,128]{2,0,1:T(8,128)S(1)} %fusion.163, f32[16,12]{0,1:T(8,128)S(1)} %fusion.282), kind=kOutput, calls=%fused_computation.358 | convolution fusion | flops 302039040 | bytes 19366656 | tf_op jit(solution)/shard_map/dot_general | solution.py:61
  145.7 9.9 %fusion.266 = f32[16,6144]{1,0:T(8,128)} fusion(bf16[1536,6144]{1,0:T(8,128)(2,1)} %param.30, f32[16,12,128]{2,0,1:T(8,128)S(1)} %fusion.162, f32[16,12]{0,1:T(8,128)S(1)} %fusion.280), kind=kOutput, calls=%fused_computation.355 | convolution fusion | flops 302039040 | bytes 19366656 | tf_op jit(solution)/shard_map/dot_general | solution.py:61
  155.7 3.3 fusion.263
  159.1 3.4 fusion.260
  162.8 70.5 %all-reduce.7.cloned.1.call-done = (f32[16,6144]{1,0:T(8,128)}, f32[16,6144]{1,0:T(8,128)}, f32[16,6144]{1,0:T(8,128)}, f32[16,6144]{1,0:T(8,128)}) async-done(((f32[16,6144]{1,0:T(8,128)}, f32[16,6144]{1,0:T(8,128)}, f32[16,6144]{1,0:T(8,128)}, f32[16,6144]{1,0:T(8,128)}), (f32[16,6144]{1,0:T(8,128)}, f32[16,6144]{1,0:T(8,128)}, f32[16,6144]{1,0:T(8,128)}, ...) | async-done | bytes 1572880 | tf_op jit(solution)/shard_map/psum | solution.py:61
  233.3 2.9 convert_reduce_fusion.3
  236.7 26.3 %fusion.125.clone.4 = bf16[16,6144]{1,0:T(8,128)(2,1)S(1)} fusion(bf16[6144,6144]{1,0:T(8,128)(2,1)} %param.36, bf16[16,6144]{1,0:T(8,128)(2,1)S(1)} %get-tuple-element.32, f32[6144]{0:T(1024)S(1)} %convert_element_type.421, f32[6144]{0:T(1024)S(1)} %convert_element_type.419, f32[6144]{0:T(1024)S(1)} %convert_element_type.418, ...), kind=kOutput, calls=%fused_computation.182.clone.clone.clone.1 | convolution fusion | flops 1209532416 | bytes 75964544 | tf_op jit(solution)/shard_map/dot_general | solution.py:33
  263.1 26.3 %fusion.136.clone.4 = bf16[16,6144]{1,0:T(8,128)(2,1)S(1)} fusion(bf16[6144,6144]{1,0:T(8,128)(2,1)} %param.36, bf16[16,6144]{1,0:T(8,128)(2,1)S(1)} %get-tuple-element.40, f32[16]{0:T(128)S(1)} %add_rsqrt_fusion.4, f32[16]{0:T(128)S(1)} %broadcast_multiply_fusion.4, f32[6144]{0:T(1024)S(1)} %convert_element_type.421, ...), kind=kOutput, calls=%fused_computation.193.clone.clone.clone.1 | convolution fusion | flops 1209532416 | bytes 75964544 | tf_op jit(solution)/shard_map/dot_general | solution.py:33
  289.4 27.0 %fusion.126 = f32[16,6144]{1,0:T(8,128)} fusion(bf16[6144,6144]{1,0:T(8,128)(2,1)} %param.38, bf16[16,6144]{1,0:T(8,128)(2,1)S(1)} %fusion.125.clone.4), kind=kOutput, calls=%fused_computation.183 | convolution fusion | flops 1207959552 | bytes 76087296 | tf_op jit(solution)/shard_map/dot_general | solution.py:65
  316.4 27.2 %fusion.137 = f32[16,6144]{1,0:T(8,128)} fusion(bf16[6144,6144]{1,0:T(8,128)(2,1)} %param.38, bf16[16,6144]{1,0:T(8,128)(2,1)S(1)} %fusion.136.clone.4), kind=kOutput, calls=%fused_computation.194 | convolution fusion | flops 1207959552 | bytes 76087296 | tf_op jit(solution)/shard_map/dot_general | solution.py:65
  343.8 26.3 %fusion.147.clone.2 = bf16[16,6144]{1,0:T(8,128)(2,1)S(1)} fusion(bf16[6144,6144]{1,0:T(8,128)(2,1)} %param.36, bf16[16,6144]{1,0:T(8,128)(2,1)S(1)} %get-tuple-element.42, f32[16]{0:T(128)S(1)} %add_rsqrt_fusion.2, f32[16]{0:T(128)S(1)} %broadcast_multiply_fusion.2, f32[6144]{0:T(1024)S(1)} %convert_element_type.421, ...), kind=kOutput, calls=%fused_computation.204.clone.clone.clone | convolution fusion | flops 1209532416 | bytes 75964544 | tf_op jit(solution)/shard_map/dot_general | solution.py:33
  370.1 27.0 %fusion.148 = f32[16,6144]{1,0:T(8,128)} fusion(bf16[6144,6144]{1,0:T(8,128)(2,1)} %param.38, bf16[16,6144]{1,0:T(8,128)(2,1)S(1)} %fusion.147.clone.2), kind=kOutput, calls=%fused_computation.205 | convolution fusion | flops 1207959552 | bytes 76087296 | tf_op jit(solution)/shard_map/dot_general | solution.py:65
  397.4 26.6 %fusion.158.clone.2 = bf16[16,6144]{1,0:T(8,128)(2,1)S(1)} fusion(bf16[6144,6144]{1,0:T(8,128)(2,1)} %param.36, bf16[16,6144]{1,0:T(8,128)(2,1)S(1)} %copy-done.13, f32[16]{0:T(128)S(1)} %add_rsqrt_fusion, f32[16]{0:T(128)S(1)} %broadcast_multiply_fusion, f32[6144]{0:T(1024)S(1)} %convert_element_type.421, ...), kind=kOutput, calls=%fused_computation.215.clone.clone.clone | convolution fusion | flops 1209532416 | bytes 75964544 | tf_op jit(solution)/shard_map/dot_general | solution.py:33
  424.0 27.0 %fusion.159 = f32[16,6144]{1,0:T(8,128)} fusion(bf16[6144,6144]{1,0:T(8,128)(2,1)} %param.38, bf16[16,6144]{1,0:T(8,128)(2,1)S(1)} %fusion.158.clone.2), kind=kOutput, calls=%fused_computation.216 | convolution fusion | flops 1207959552 | bytes 76087296 | tf_op jit(solution)/shard_map/dot_general | solution.py:65
  451.0 68.5 %all-reduce.5.cloned.1.call-done = (f32[16,6144]{1,0:T(8,128)}, f32[16,6144]{1,0:T(8,128)}, f32[16,6144]{1,0:T(8,128)}, f32[16,6144]{1,0:T(8,128)}) async-done(((f32[16,6144]{1,0:T(8,128)}, f32[16,6144]{1,0:T(8,128)}, f32[16,6144]{1,0:T(8,128)}, f32[16,6144]{1,0:T(8,128)}), (f32[16,6144]{1,0:T(8,128)}, f32[16,6144]{1,0:T(8,128)}, f32[16,6144]{1,0:T(8,128)}, ...) | async-done | bytes 1572880 | tf_op jit(solution)/shard_map/psum | solution.py:65
  519.5 1.5 fusion.167
  521.0 1.0 pad_maximum_fusion
  (171 shorter events, 13.4 us)
Async XLA Ops:
  7.2 7.8 %copy-start = (bf16[6144,128]{1,0:T(8,128)(2,1)S(1)}, bf16[6144,128]{1,0:T(8,128)(2,1)}, u32[]{:S(2)}) copy-start(bf16[6144,128]{1,0:T(8,128)(2,1)} %param.26) | copy-start | bytes 4718596
  7.2 226.1 %all-reduce.7.cloned.1.call-start = ((), (), s32[]{:S(2)}) async-start(), calls=%async_computation.1 | async-start | bytes 3145728 | tf_op jit(solution)/shard_map/psum | solution.py:61
  7.2 4.8 copy-start.8
  12.0 2.1 copy-start.21
  12.0 2.1 copy-start.6
  12.0 2.8 copy-start.14
  12.0 2.8 copy-start.15
  12.0 2.8 copy-start.24
  12.0 2.9 copy-start.22
  15.7 18.1 %slice-start = ((s8[18874368]{0:T(1024)(128)(4,1)}), s8[4194304]{0:T(1024)(128)(4,1)S(1)}, s32[]{:S(2)}) async-start(s8[18874368]{0:T(1024)(128)(4,1)} %bitcast.326), calls=%async_computation.2 | async-start | bytes 8388608
  15.7 18.1 %slice-start.1 = ((s8[18874368]{0:T(1024)(128)(4,1)}), s8[4194304]{0:T(1024)(128)(4,1)S(1)}, s32[]{:S(2)}) async-start(s8[18874368]{0:T(1024)(128)(4,1)} %bitcast.326), calls=%async_computation.3 | async-start | bytes 8388608
  15.7 18.1 %slice-start.2 = ((s8[18874368]{0:T(1024)(128)(4,1)}), s8[4194304]{0:T(1024)(128)(4,1)S(1)}, s32[]{:S(2)}) async-start(s8[18874368]{0:T(1024)(128)(4,1)} %bitcast.326), calls=%async_computation.4 | async-start | bytes 8388608
  23.6 9.0 %copy-start.25 = (bf16[128]{0:T(256)(128)(2,1)S(1)}, bf16[128]{0:T(256)(128)(2,1)}, u32[]{:S(2)}) copy-start(bf16[128]{0:T(256)(128)(2,1)} %param.29) | copy-start | bytes 772
  23.6 9.0 %copy-start.7 = (bf16[6144,128]{1,0:T(8,128)(2,1)S(1)}, bf16[6144,128]{1,0:T(8,128)(2,1)}, u32[]{:S(2)}) copy-start(bf16[6144,128]{1,0:T(8,128)(2,1)} %param.28) | copy-start | bytes 4718596
  23.6 10.2 %slice-start.3 = ((s8[18874368]{0:T(1024)(128)(4,1)}), s8[4194304]{0:T(1024)(128)(4,1)S(1)}, s32[]{:S(2)}) async-start(s8[18874368]{0:T(1024)(128)(4,1)} %bitcast.326), calls=%async_computation.5 | async-start | bytes 8388608
  23.6 10.2 %slice-start.4 = ((s8[18874368]{0:T(1024)(128)(4,1)}), s8[2097152]{0:T(1024)(128)(4,1)S(1)}, s32[]{:S(2)}) async-start(s8[18874368]{0:T(1024)(128)(4,1)} %bitcast.326), calls=%async_computation.6 | async-start | bytes 4194304
  45.5 4.7 copy-start.2
  78.9 4.2 copy-start.3
  99.4 4.2 copy-start.4
  119.9 4.2 copy-start.5
  135.7 19.9 %slice-start.5 = ((s8[18874368]{0:T(1024)(128)(4,1)}), s8[4194304]{0:T(1024)(128)(4,1)S(1)}, s32[]{:S(2)}) async-start(s8[18874368]{0:T(1024)(128)(4,1)} %bitcast.328), calls=%async_computation.7 | async-start | bytes 8388608
  135.8 19.9 %slice-start.6 = ((s8[18874368]{0:T(1024)(128)(4,1)}), s8[4194304]{0:T(1024)(128)(4,1)S(1)}, s32[]{:S(2)}) async-start(s8[18874368]{0:T(1024)(128)(4,1)} %bitcast.328), calls=%async_computation.8 | async-start | bytes 8388608
  135.8 19.9 %slice-start.7 = ((s8[18874368]{0:T(1024)(128)(4,1)}), s8[4194304]{0:T(1024)(128)(4,1)S(1)}, s32[]{:S(2)}) async-start(s8[18874368]{0:T(1024)(128)(4,1)} %bitcast.328), calls=%async_computation.9 | async-start | bytes 8388608
  145.6 10.0 %slice-start.8 = ((s8[18874368]{0:T(1024)(128)(4,1)}), s8[4194304]{0:T(1024)(128)(4,1)S(1)}, s32[]{:S(2)}) async-start(s8[18874368]{0:T(1024)(128)(4,1)} %bitcast.328), calls=%async_computation.10 | async-start | bytes 8388608
  145.6 10.0 %slice-start.9 = ((s8[18874368]{0:T(1024)(128)(4,1)}), s8[2097152]{0:T(1024)(128)(4,1)S(1)}, s32[]{:S(2)}) async-start(s8[18874368]{0:T(1024)(128)(4,1)} %bitcast.328), calls=%async_computation.11 | async-start | bytes 4194304
  159.0 3.6 copy-start.16
  159.0 3.7 copy-start.17
  159.1 3.7 copy-start.18
  159.1 3.7 copy-start.19
  162.5 357.0 %all-reduce.5.cloned.1.call-start = ((), (), s32[]{:S(2)}) async-start(), calls=%async_computation | async-start | bytes 3145728 | tf_op jit(solution)/shard_map/psum | solution.py:65
  236.2 26.8 %copy-start.9 = (bf16[16,6144]{1,0:T(8,128)(2,1)}, bf16[16,6144]{1,0:T(8,128)(2,1)S(1)}, u32[]{:S(2)}) copy-start(bf16[16,6144]{1,0:T(8,128)(2,1)S(1)} %get-tuple-element.32) | copy-start | bytes 589828
  236.2 26.9 %copy-start.11 = (bf16[16,6144]{1,0:T(8,128)(2,1)}, bf16[16,6144]{1,0:T(8,128)(2,1)S(1)}, u32[]{:S(2)}) copy-start(bf16[16,6144]{1,0:T(8,128)(2,1)S(1)} %get-tuple-element.40) | copy-start | bytes 589828
  370.1 27.0 %copy-start.23 = (f32[16]{0:T(128)S(1)}, f32[16]{0:T(128)}, u32[]{:S(2)}) copy-start(f32[16]{0:T(128)} %get-tuple-element.43) | copy-start | bytes 196
  370.1 27.0 %copy-start.13 = (bf16[16,6144]{1,0:T(8,128)(2,1)S(1)}, bf16[16,6144]{1,0:T(8,128)(2,1)}, u32[]{:S(2)}) copy-start(bf16[16,6144]{1,0:T(8,128)(2,1)} %get-tuple-element.44) | copy-start | bytes 589828
  424.0 27.1 %copy-start.20 = (bf16[6144]{0:T(1024)(128)(2,1)S(1)}, bf16[6144]{0:T(1024)(128)(2,1)}, u32[]{:S(2)}) copy-start(bf16[6144]{0:T(1024)(128)(2,1)} %param.39) | copy-start | bytes 36868
  424.0 95.5 %copy-start.10 = (bf16[16,6144]{1,0:T(8,128)(2,1)S(1)}, bf16[16,6144]{1,0:T(8,128)(2,1)}, u32[]{:S(2)}) copy-start(bf16[16,6144]{1,0:T(8,128)(2,1)} %copy-done.9) | copy-start | bytes 589828
  424.0 95.5 %copy-start.12 = (bf16[16,6144]{1,0:T(8,128)(2,1)S(1)}, bf16[16,6144]{1,0:T(8,128)(2,1)}, u32[]{:S(2)}) copy-start(bf16[16,6144]{1,0:T(8,128)(2,1)} %copy-done.11) | copy-start | bytes 589828
  424.0 98.0 %copy-start.1 = (bf16[6144,128]{1,0:T(8,128)(2,1)S(1)}, bf16[6144,128]{1,0:T(8,128)(2,1)}, u32[]{:S(2)}) copy-start(bf16[6144,128]{1,0:T(8,128)(2,1)} %param.26) | copy-start | bytes 4718596
Sparse Core Ops, SparseCore 0:
  162.6 70.6 all-reduce.6
  451.1 68.3 all-reduce.4
where the time goes:
time: 534 us; the launch traced here: 529 us
  matrix products  283 us (53%)
  waiting for transfers between devices  139 us (26%)
  blocking collectives  46.4 us (9%)
  local copies, waits for them, and re-layouts  30.2 us (6%)
  between operations  15.4 us (3%)
  other arithmetic  15.1 us (3%)
    dot_general x16, matrix products, linear(): jnp.dot(rows_in, weight, preferred_element_type=jnp.float32)  131 us
    dot_general x4, matrix products, layer_tail(): jnp.dot(gelu_out, w_proj, preferred_element_type=jnp.float32)  108 us
    psum x1, waiting for transfers between devices, layer_tail(): lax.psum(jnp.dot(attn_out, w_o, preferred_element_type=jnp.float32), 'tp')  70.5 us
    psum x1, waiting for transfers between devices, layer_tail(): lax.psum(jnp.dot(gelu_out, w_proj, preferred_element_type=jnp.float32), '...  68.5 us
    all_gather x4, blocking collectives, per_device(): gathered = lax.all_gather(stats, 'sq')  46.4 us
    dot_general x4, matrix products, layer_tail(): jnp.dot(attn_out, w_o, preferred_element_type=jnp.float32)  26.5 us
    dot_general x4, matrix products, partial_attention(): jnp.einsum('bgrd,bwgd->bgrw', q_rot, key_buf, preferred_element_type=jnp....  14.8 us
  transfers between devices with their start and end apart: 2, of which 2 were waited for; matrix products, arithmetic and copies ran while one was open for 0% of the time, Pallas kernels for 0%

commit v1 on v0

v1 whole, which is shorter than its diff:
```python
import functools

import jax
import jax.numpy as jnp
from jax import lax
from jax.experimental import pallas as pl
from jax.experimental.pallas import tpu as pltpu
from jax.sharding import PartitionSpec as P

ROPE_BASE = 1000000.0
LN_EPS = 1e-5
NEG_BIG = -1e30
MESH = pl.DeviceIdType.MESH

NCH = 6
CW = 512
NSUB = 6
NSLOT = 14


def layer_norm(vectors, gain, shift):
    row_mean = jnp.mean(vectors, axis=-1, keepdims=True)
    centered = vectors - row_mean
    row_var = jnp.mean(centered * centered, axis=-1, keepdims=True)
    return centered * lax.rsqrt(row_var + LN_EPS) * gain.astype(jnp.float32) + shift.astype(jnp.float32)


def rope_tables(positions, head_dim):
    half_dim = head_dim // 2
    inv_freq = jnp.power(jnp.float32(ROPE_BASE), -2.0 * jnp.arange(half_dim, dtype=jnp.float32) / head_dim)
    angle = positions.astype(jnp.float32)[..., None] * inv_freq
    return jnp.cos(angle), jnp.sin(angle)


def apply_rope(vectors, cos_t, sin_t):
    half_dim = vectors.shape[-1] // 2
    first = vectors[..., :half_dim]
    second = vectors[..., half_dim:]
    return jnp.concatenate([first * cos_t - second * sin_t, second * cos_t + first * sin_t], axis=-1)


def linear(rows_in, weight, bias):
    return jnp.dot(rows_in, weight, preferred_element_type=jnp.float32) + bias.astype(jnp.float32)


def tail_kernel(part, x_hbm, vecs, wo, wfc, wproj, out,
                rx, abuf, wobuf, wbuf, xbuf, mm1, dr1, cs1, cr1, x1buf, stat, hbuf, acc, gbuf,
                mm2, dr2, cs2, cr2, ybuf,
                wo_sem, w_sem, x_sem, rx_s, rx_r,
                d1_s, d1_r, c1_s, c1_r, st_s, st_r, h_cs, h_ds, h_r,
                d2_s, d2_r, c2_s, c2_r, y_cs, y_ds, y_ys, y_r):
    dp, z, sq = lax.axis_index("dp"), lax.axis_index("tp"), lax.axis_index("sq")
    y, c = sq // 2, sq % 2
    hw = NCH * CW
    pos = z + c * (3 - 2 * z)
    nxt = z + 1 - 2 * c
    prv = z - 1 + 2 * c
    f = z // 2
    own_first = c == f
    chip_core = (dp, z, 2 * y + 1 - c)
    chip_y = (dp, z, 2 * (1 - y) + c)
    chip_yc = (dp, z, 2 * (1 - y) + 1 - c)
    up = (dp, nxt, sq)
    down = (dp, prv, sq)
    stat_peer = (dp, 3 - z, 2 * y + 1 - c)

    def wo_copy(k):
        hs = jnp.where(k < NCH, f, 1 - f)
        j = k % NCH
        col = pl.multiple_of(hs * hw + j * CW, CW)
        return pltpu.make_async_copy(wo.at[pl.ds(pl.multiple_of(c * 768, 768), 768), pl.ds(col, CW)], wobuf.at[k], wo_sem.at[k])

    def fc_copy(k, i):
        hs = jnp.where(k < NCH, 1 - f, f)
        j = k % NCH
        row = pl.multiple_of(hs * hw + j * CW, CW)
        col = pl.multiple_of(c * hw + i * CW, CW)
        return pltpu.make_async_copy(wfc.at[pl.ds(row, CW), pl.ds(col, CW)], wbuf.at[k, i], w_sem.at[k, i])

    def pj_copy(k, i):
        slot = (k + 2 * NCH) % NSLOT
        hs = jnp.where(k < NCH, f, 1 - f)
        j = k % NCH
        row = pl.multiple_of(c * hw + i * CW, CW)
        col = pl.multiple_of(hs * hw + j * CW, CW)
        return pltpu.make_async_copy(wproj.at[pl.ds(row, CW), pl.ds(col, CW)], wbuf.at[slot, i], w_sem.at[slot, i])

    def x_copy():
        return pltpu.make_async_copy(x_hbm.at[pl.ds(2 * y, 2), :, pl.ds(pl.multiple_of(c * hw, hw), hw)], xbuf, x_sem)

    x_copy().start()

    @pl.loop(0, 2 * NCH)
    def _(k):
        wo_copy(k).start()

    @pl.loop(0, 2 * NCH)
    def _(k):
        for i in range(NSUB):
            fc_copy(k, i).start()

    @pl.loop(0, NSLOT - 2 * NCH)
    def _(k):
        for i in range(NSUB):
            pj_copy(k, i).start()

    bar = pltpu.get_barrier_semaphore()
    for dev in (chip_core, chip_y, chip_yc):
        pl.semaphore_signal(bar, inc=1, device_id=dev, device_id_type=MESH)

    @pl.when(pos < 3)
    def _():
        pl.semaphore_signal(bar, inc=1, device_id=up, device_id_type=MESH)

    @pl.when(pos > 0)
    def _():
        pl.semaphore_signal(bar, inc=1, device_id=down, device_id_type=MESH)

    @pl.when(pos == 3)
    def _():
        pl.semaphore_signal(bar, inc=1, device_id=stat_peer, device_id_type=MESH)
        pl.semaphore_wait(bar, 5)

    @pl.when(pos == 0)
    def _():
        pl.semaphore_wait(bar, 4)

    @pl.when((pos == 1) | (pos == 2))
    def _():
        pl.semaphore_wait(bar, 5)

    def remote(src, dst, ssem, rsem, dev):
        return pltpu.make_async_remote_copy(src_ref=src, dst_ref=dst, send_sem=ssem, recv_sem=rsem, device_id=dev, device_id_type=MESH)

    peers = (chip_y, chip_yc, chip_core)
    for n, dev in enumerate(peers):
        remote(part.at[dev[2]], rx.at[n], rx_s.at[n], rx_r.at[n], dev).start()
    for n, dev in enumerate(peers):
        remote(part.at[dev[2]], rx.at[n], rx_s.at[n], rx_r.at[n], dev).wait()
    stats = [part[sq, :, 768:896]] + [rx[n, :, 768:896] for n in range(3)]
    top = functools.reduce(jnp.maximum, stats)
    scale = [jnp.exp(s - top) for s in stats]
    for h in range(6):
        cols = slice(h * 128, (h + 1) * 128)
        outs = [part[sq, :, cols]] + [rx[n, :, cols] for n in range(3)]
        num = sum(o * r[:, h:h + 1] for o, r in zip(outs, scale))
        den = sum(s[:, 64 + h:65 + h] * r[:, h:h + 1] for s, r in zip(stats, scale))
        abuf[:, cols] = (num / den).astype(jnp.bfloat16)

    def reduce_chunks(product, mm, dr, cs, cr, d_s, d_r, c_s, c_r, finish):
        for phase in range(2):
            own = own_first if phase == 0 else jnp.logical_not(own_first)

            @pl.loop(0, NCH)
            def _(j):
                k = j + phase * NCH
                mm[k] = product(k)

                @pl.when(jnp.logical_not(own))
                def _():
                    remote(mm.at[k], dr.at[j], d_s.at[j], d_r.at[j], chip_core).start()

                @pl.when(own)
                def _():
                    remote(mm.at[k], dr.at[j], d_s.at[j], d_r.at[j], chip_core).wait_recv()
                    if phase == 0:
                        @pl.when(pos == 0)
                        def _():
                            cs[j] = mm[k] + dr[j]

                        @pl.when(pos == 1)
                        def _():
                            remote(cs.at[j], cr.at[j], c_s.at[j], c_r.at[j], up).wait_recv()
                            cs[j] = mm[k] + dr[j] + cr[j]

                        remote(cs.at[j], cr.at[j], c_s.at[j], c_r.at[j], up).start()
                    else:
                        remote(cs.at[j], cr.at[j], c_s.at[j], c_r.at[j], down).wait_recv()
                        total = mm[k] + dr[j] + cr[j]

                        @pl.when(pos == 2)
                        def _():
                            cs[j] = total
                            remote(cs.at[j], cr.at[j], c_s.at[j], c_r.at[j], up).start()

                        @pl.when(pos == 3)
                        def _():
                            finish(j, total)

    def vec(row, start):
        return vecs[pl.ds(row, 1), pl.ds(pl.multiple_of(start, CW), CW)]

    def wo_product(k):
        wo_copy(k).wait()
        return jnp.dot(abuf[...], wobuf[k], preferred_element_type=jnp.float32)

    def wo_finish(j, total):
        x_in = xbuf[:, :, pl.ds(pl.multiple_of(j * CW, CW), CW)].astype(jnp.float32).reshape(32, CW)
        x1buf[j] = (x_in + total + vec(0, c * hw + j * CW)).astype(jnp.bfloat16).astype(jnp.float32)

    x_copy().wait()
    reduce_chunks(wo_product, mm1, dr1, cs1, cr1, d1_s, d1_r, c1_s, c1_r, wo_finish)

    @pl.when(pos == 3)
    def _():
        mean = sum(jnp.sum(x1buf[j], axis=-1, keepdims=True) for j in range(NCH)) / hw
        m2 = 0.0
        for j in range(NCH):
            cen = x1buf[j] - mean
            m2 = m2 + jnp.sum(cen * cen, axis=-1, keepdims=True)
        lane = lax.broadcasted_iota(jnp.int32, (32, 128), 1)
        stat[0] = jnp.where(lane < 64, jnp.broadcast_to(mean, (32, 128)), jnp.broadcast_to(m2, (32, 128)))
        cp = remote(stat.at[0], stat.at[1], st_s, st_r, stat_peer)
        cp.start()
        cp.wait()
        mean_b, m2_b = stat[1, :, 0:1], stat[1, :, 64:65]
        diff = mean - mean_b
        row_mean = 0.5 * (mean + mean_b)
        row_var = (m2 + m2_b + diff * diff * (0.5 * hw)) / (2.0 * hw)
        inv = lax.rsqrt(row_var + LN_EPS)
        for j in range(NCH):
            hid = (x1buf[j] - row_mean) * inv * vec(1, c * hw + j * CW) + vec(2, c * hw + j * CW)
            hbuf[c, j] = hid.astype(jnp.bfloat16).astype(jnp.float32)
            remote(hbuf.at[c, j], hbuf.at[c, j], h_cs.at[j], h_r.at[c, j], down).start()
            remote(hbuf.at[c, j], hbuf.at[c, j], h_ds.at[j], h_r.at[c, j], chip_core).start()

    for i in range(NSUB):
        acc[:, i * CW:(i + 1) * CW] = jnp.broadcast_to(vec(4, c * hw + i * CW), (32, CW))

    def h_arrive(half, j):
        remote(hbuf.at[half, j], hbuf.at[half, j], h_cs.at[j], h_r.at[half, j], chip_core).wait_recv()

    def h_pass_down(j):
        remote(hbuf.at[c, j], hbuf.at[c, j], h_cs.at[j], h_r.at[c, j], down).start()

    def h_pass_core(j):
        remote(hbuf.at[c, j], hbuf.at[c, j], h_ds.at[j], h_r.at[c, j], chip_core).start()

    for phase in range(2):
        half = 1 - f if phase == 0 else f

        @pl.loop(0, NCH)
        def _(j):
            k = j + phase * NCH
            if phase == 0:
                @pl.when(own_first)
                def _():
                    h_arrive(1 - c, j)

                @pl.when(pos == 2)
                def _():
                    h_arrive(c, j)
                    h_pass_down(j)
                    h_pass_core(j)

                @pl.when((pos == 1) & (j >= 2))
                def _():
                    h_arrive(c, j - 2)
                    h_pass_down(j - 2)
                    h_pass_core(j - 2)
            else:
                @pl.when(jnp.logical_not(own_first))
                def _():
                    h_arrive(1 - c, j)

                @pl.when(pos == 0)
                def _():
                    h_arrive(c, j)
                    h_pass_core(j)

                @pl.when((pos == 1) & (j >= NCH - 2))
                def _():
                    h_arrive(c, j)
                    h_pass_down(j)
                    h_pass_core(j)

            for i in range(NSUB):
                fc_copy(k, i).wait()
            hid = hbuf[half, j].astype(jnp.bfloat16)
            for i in range(NSUB):
                cols = slice(i * CW, (i + 1) * CW)
                acc[:, cols] += jnp.dot(hid, wbuf[k, i], preferred_element_type=jnp.float32)

            @pl.when(k < 2 * NCH - (NSLOT - 2 * NCH))
            def _():
                for i in range(NSUB):
                    pj_copy(k + NSLOT - 2 * NCH, i).start()

    for i in range(NSUB):
        cols = slice(i * CW, (i + 1) * CW)
        gbuf[:, cols] = jax.nn.gelu(acc[:, cols], approximate=True).astype(jnp.bfloat16)

    def pj_product(k):
        slot = (k + 2 * NCH) % NSLOT
        for i in range(NSUB):
            pj_copy(k, i).wait()
        return sum(jnp.dot(gbuf[:, i * CW:(i + 1) * CW], wbuf[slot, i], preferred_element_type=jnp.float32) for i in range(NSUB))

    def y_pass_down(j):
        remote(ybuf.at[y, c, j], ybuf.at[y, c, j], y_cs.at[j], y_r.at[y, c, j], down).start()

    def y_pass_across(j):
        remote(ybuf.at[y, c, j], ybuf.at[y, c, j], y_ys.at[j], y_r.at[y, c, j], chip_y).start()

    def y_pass_core(side, j):
        remote(ybuf.at[side, c, j], ybuf.at[side, c, j], y_ds.at[side, j], y_r.at[side, c, j], chip_core).start()

    def y_arrive(side, half, j):
        remote(ybuf.at[side, half, j], ybuf.at[side, half, j], y_cs.at[j], y_r.at[side, half, j], chip_core).wait_recv()

    def pj_finish(j, total):
        ybuf[y, c, j] = (x1buf[j] + total + vec(3, c * hw + j * CW)).astype(jnp.bfloat16).astype(jnp.float32)
        y_pass_down(j)
        y_pass_across(j)
        y_pass_core(y, j)

    reduce_chunks(pj_product, mm2, dr2, cs2, cr2, d2_s, d2_r, c2_s, c2_r, pj_finish)

    def emit(side, half, j):
        col = pl.multiple_of(half * hw + j * CW, CW)
        out[pl.ds(2 * side, 2), :, pl.ds(col, CW)] = ybuf[side, half, j].reshape(2, 16, CW).astype(jnp.bfloat16)

    for j in range(NCH + 2):
        if j < NCH:
            @pl.when(pos < 3)
            def _():
                y_arrive(y, c, j)

                @pl.when(pos > 0)
                def _():
                    y_pass_down(j)

                y_pass_across(j)
                y_pass_core(y, j)

            emit(y, c, j)
        if j >= 2:
            y_arrive(1 - y, c, j - 2)
            y_pass_core(1 - y, j - 2)
            emit(1 - y, c, j - 2)

    @pl.loop(0, NCH)
    def _(j):
        y_arrive(y, 1 - c, j)
        emit(y, 1 - c, j)
        y_arrive(1 - y, 1 - c, j)
        emit(1 - y, 1 - c, j)

    @pl.loop(0, NCH)
    def _(j):
        remote(mm1.at[j], dr1.at[j], d1_s.at[j], d1_r.at[j], chip_core).wait_send()
        remote(mm2.at[j], dr2.at[j], d2_s.at[j], d2_r.at[j], chip_core).wait_send()
        remote(hbuf.at[c, j], hbuf.at[c, j], h_ds.at[j], h_r.at[c, j], chip_core).wait_send()
        remote(ybuf.at[y, c, j], ybuf.at[y, c, j], y_ys.at[j], y_r.at[y, c, j], chip_y).wait_send()
        for side in range(2):
            remote(ybuf.at[side, c, j], ybuf.at[side, c, j], y_ds.at[side, j], y_r.at[side, c, j], chip_core).wait_send()

        @pl.when(pos < 3)
        def _():
            remote(cs1.at[j], cr1.at[j], c1_s.at[j], c1_r.at[j], up).wait_send()
            remote(cs2.at[j], cr2.at[j], c2_s.at[j], c2_r.at[j], up).wait_send()

        @pl.when(pos > 0)
        def _():
            remote(hbuf.at[c, j], hbuf.at[c, j], h_cs.at[j], h_r.at[c, j], down).wait_send()
            remote(ybuf.at[y, c, j], ybuf.at[y, c, j], y_cs.at[j], y_r.at[y, c, j], down).wait_send()


def layer_tail(part, x_steps, vecs, w_o, w_fc, w_proj):
    hbm = pl.BlockSpec(memory_space=pltpu.HBM)
    vmem = pl.BlockSpec(memory_space=pltpu.VMEM)
    f32, bf16 = jnp.float32, jnp.bfloat16
    chunks = pltpu.VMEM((NCH, 32, CW), f32)
    dma = pltpu.SemaphoreType.DMA
    return pl.pallas_call(
        tail_kernel,
        out_shape=jax.ShapeDtypeStruct(x_steps.shape, bf16),
        in_specs=[vmem, hbm, vmem, hbm, hbm, hbm],
        out_specs=vmem,
        scratch_shapes=[
            pltpu.VMEM((3, 32, 896), f32), pltpu.VMEM((32, 768), bf16), pltpu.VMEM((2 * NCH, 768, CW), bf16),
            pltpu.VMEM((NSLOT, NSUB, CW, CW), bf16), pltpu.VMEM((2, 16, NCH * CW), bf16),
            pltpu.VMEM((2 * NCH, 32, CW), f32), chunks, chunks, chunks, chunks, pltpu.VMEM((2, 32, 128), f32),
            pltpu.VMEM((2, NCH, 32, CW), f32), pltpu.VMEM((32, NCH * CW), f32), pltpu.VMEM((32, NCH * CW), bf16),
            pltpu.VMEM((2 * NCH, 32, CW), f32), chunks, chunks, chunks, pltpu.VMEM((2, 2, NCH, 32, CW), f32),
            dma((2 * NCH,)), dma((NSLOT, NSUB)), dma, dma((3,)), dma((3,)),
            dma((NCH,)), dma((NCH,)), dma((NCH,)), dma((NCH,)), dma, dma, dma((NCH,)), dma((NCH,)), dma((2, NCH)),
            dma((NCH,)), dma((NCH,)), dma((NCH,)), dma((NCH,)), dma((NCH,)), dma((2, NCH)), dma((NCH,)), dma((2, 2, NCH)),
        ],
        compiler_params=pltpu.CompilerParams(collective_id=0, has_side_effects=True, vmem_limit_bytes=67043328),
    )(part, x_steps, vecs, w_o, w_fc, w_proj)


def attention_parts(x_steps, positions, k_cache, v_cache, w_q, b_q, w_k, b_k, w_v, b_v, ln1_gain, ln1_bias, sq_size):
    steps, batch, width = x_steps.shape
    slots_local, head_dim = k_cache.shape[1], k_cache.shape[3]
    heads = w_q.shape[1] // head_dim
    slots = slots_local * sq_size
    first_slot = lax.axis_index("sq") * slots_local
    slot_ids = first_slot + jnp.arange(slots_local, dtype=jnp.int32)
    step_ids = jnp.arange(steps, dtype=jnp.int32)
    hidden = layer_norm(x_steps.astype(jnp.float32), ln1_gain, ln1_bias).astype(jnp.bfloat16).reshape(steps * batch, width)
    query = linear(hidden, w_q, b_q).astype(jnp.bfloat16).reshape(steps, batch, heads, head_dim)
    key_new = linear(hidden, w_k, b_k).astype(jnp.bfloat16).reshape(steps, batch, head_dim)
    val_new = linear(hidden, w_v, b_v).astype(jnp.bfloat16).reshape(steps, batch, head_dim)
    cos_t, sin_t = rope_tables(positions[None, :] + step_ids[:, None], head_dim)
    q_rot = apply_rope(query.astype(jnp.float32), cos_t[:, :, None, :], sin_t[:, :, None, :]).astype(jnp.bfloat16)
    k_rot = apply_rope(key_new.astype(jnp.float32), cos_t, sin_t).astype(jnp.bfloat16)
    q_all = q_rot.transpose(1, 0, 2, 3).reshape(batch, steps * heads, head_dim)
    k_all, v_all = k_rot.transpose(1, 0, 2), val_new.transpose(1, 0, 2)
    age = (positions[:, None] - 1 - slot_ids[None, :]) % slots
    limit = jnp.minimum(positions[:, None] - 1, slots - 2 - step_ids[None, :])
    row_limit = jnp.repeat(limit, heads, axis=1)
    old_ok = age[:, None, :] <= row_limit[:, :, None]
    write_slot = (positions[:, None] + step_ids[None, :]) % slots - first_slot
    is_here = (write_slot >= 0) & (write_slot < slots_local)
    row_step = jnp.repeat(step_ids, heads)
    new_ok = is_here[:, None, :] & (step_ids[None, None, :] <= row_step[None, :, None])
    scale = head_dim ** -0.5
    k_old, v_old = k_cache[:, :, 0], v_cache[:, :, 0]
    s_old = jnp.where(old_ok, jnp.einsum("brd,bwd->brw", q_all, k_old, preferred_element_type=jnp.float32) * scale, NEG_BIG)
    s_new = jnp.where(new_ok, jnp.einsum("brd,bwd->brw", q_all, k_all, preferred_element_type=jnp.float32) * scale, NEG_BIG)
    top = jnp.maximum(jnp.max(s_old, axis=-1), jnp.max(s_new, axis=-1))
    w_old = jnp.where(old_ok, jnp.exp(s_old - top[..., None]), 0.0)
    w_new = jnp.where(new_ok, jnp.exp(s_new - top[..., None]), 0.0)
    total = jnp.sum(w_old, axis=-1) + jnp.sum(w_new, axis=-1)
    part = jnp.einsum("brw,bwd->brd", w_old.astype(jnp.bfloat16), v_old, preferred_element_type=jnp.float32)
    part = part + jnp.einsum("brw,bwd->brd", w_new.astype(jnp.bfloat16), v_all, preferred_element_type=jnp.float32)

    def arrange(t):
        n = t.shape[-1]
        return t.reshape(batch, 2, 2, 2, heads // 2, n).transpose(1, 3, 2, 0, 4, 5)

    outs = arrange(part).reshape(4, 32, 768)
    tops = arrange(top[..., None]).reshape(4, 32, 6)
    sums = arrange(total[..., None]).reshape(4, 32, 6)
    pad = ((0, 0), (0, 0), (0, 58))
    packed = jnp.concatenate([outs, jnp.pad(tops, pad), jnp.pad(sums, pad)], axis=-1)
    k_out, v_out = k_cache, v_cache
    target = jnp.where(is_here, write_slot, slots_local)
    batch_ids = jnp.arange(batch, dtype=jnp.int32)
    k_out = k_out.at[batch_ids[:, None], target].set(k_all[:, :, None, :], mode="drop")
    v_out = v_out.at[batch_ids[:, None], target].set(v_all[:, :, None, :], mode="drop")
    return packed, k_out, v_out


def solution(mesh):
    sq_size = mesh.shape["sq"]
    act_spec = P(None, "dp", None)
    cache_spec = P("dp", "sq", "tp", None)
    col_spec = P(None, "tp")
    row_spec = P("tp", None)
    vec_spec = P("tp")
    rep_spec = P(None)
    in_specs = (act_spec, P("dp"), cache_spec, cache_spec, col_spec, vec_spec, col_spec, vec_spec,
                col_spec, vec_spec, row_spec, rep_spec, rep_spec, rep_spec, rep_spec, rep_spec,
                col_spec, vec_spec, row_spec, rep_spec)
    out_specs = (act_spec, cache_spec, cache_spec)

    def per_device(x_steps, positions, k_cache, v_cache, w_q, b_q, w_k, b_k, w_v, b_v, w_o, b_o,
                   ln1_gain, ln1_bias, ln2_gain, ln2_bias, w_fc, b_fc, w_proj, b_proj):
        part, k_out, v_out = attention_parts(x_steps, positions, k_cache, v_cache, w_q, b_q, w_k, b_k, w_v, b_v,
                                             ln1_gain, ln1_bias, sq_size)
        vecs = jnp.stack([b_o, ln2_gain, ln2_bias, b_proj, b_fc, b_fc, b_fc, b_fc]).astype(jnp.float32)
        ys = layer_tail(part, x_steps, vecs, w_o, w_fc, w_proj)
        return ys, k_out, v_out

    return jax.shard_map(per_device, mesh=mesh, in_specs=in_specs, out_specs=out_specs, check_vma=False)
```

time: 534 us -> 131 us (0.25)
  matrix products: 283 us -> 16.4 us
  waiting for transfers between devices: 139 us -> 0 us
  Pallas kernels: 0 us -> 82 us
  blocking collectives: 46.4 us -> 0 us
  between operations: 15.4 us -> 1.08 us
  other arithmetic: 15.1 us -> 4.71 us
    dot_general x16 -> x4, matrix products: 152 us -> 7.38 us  [the longest x1 3.84 us: attention_parts(): jnp.einsum('brd,bwd->brw', q_all, k_old, preferred_element_type=jnp.float32)]
    psum x2 -> x0, waiting for transfers between devices: 139 us -> none  [the longest x1 70.5 us: layer_tail(): lax.psum(jnp.dot(attn_out, w_o, preferred_element_type=jnp.float32), 'tp')]
    dot_general x16 -> x3, matrix products: 131 us -> 8.99 us  [linear(): jnp.dot(rows_in, weight, preferred_element_type=jnp.float32)]
    pallas_call x0 -> x1, Pallas kernels: none -> 82 us  [layer_tail(): pl.pallas_call(tail_kernel, out_shape=jax.ShapeDtypeStruct(x_steps.shape,...]
    all_gather x4 -> x0, blocking collectives: 46.4 us -> none  [per_device(): gathered = lax.all_gather(stats, 'sq')]
    scatter x8 -> x2, local copies, waits for them, and re-layouts: 20 us -> 16.2 us  [the longest x1 8.12 us: attention_parts(): k_out.at[batch_ids[:, None], target].set(k_all[:, :, None, :], mode='drop')]
  transfers between devices with their start and end apart: 2 -> 0, of which waited for: 2 -> 0; matrix products, arithmetic and copies ran while one was open for 0% -> 0% of each run, Pallas kernels for 0% -> 0%
where the time goes in v1:
time: 131 us
  Pallas kernels  82 us (63%)
  local copies, waits for them, and re-layouts  26.8 us (20%)
  matrix products  16.4 us (13%)
  other arithmetic  4.71 us (4%)
    pallas_call x1, Pallas kernels, layer_tail(): pl.pallas_call(tail_kernel, out_shape=jax.ShapeDtypeStruct(x_steps.shape,...  82 us
    dot_general x3, matrix products, linear(): jnp.dot(rows_in, weight, preferred_element_type=jnp.float32)  8.99 us
    unnamed x33, local copies, waits for them, and re-layouts  8.92 us
    scatter x1, local copies, waits for them, and re-layouts, attention_parts(): k_out.at[batch_ids[:, None], target].set(k_all[:, :, None, :], mode='drop')  8.12 us
    scatter x1, local copies, waits for them, and re-layouts, attention_parts(): v_out.at[batch_ids[:, None], target].set(v_all[:, :, None, :], mode='drop')  8.12 us
    dot_general x1, matrix products, attention_parts(): jnp.einsum('brd,bwd->brw', q_all, k_old, preferred_element_type=jnp.float32)  3.84 us
    dot_general x1, matrix products, attention_parts(): jnp.einsum('brw,bwd->brd', w_old.astype(jnp.bfloat16), v_old, preferred_e...  2.89 us

profile of v1, /device:TPU:0, one launch (start us, length us, event | category | flops | bytes accessed | tf_op | source)
XLA Modules:
  0.0 130.9 jit_solution(6333249743384261442)
XLA Ops:
  0.6 4.8 %copy.103 = bf16[16,1024,1,128]{3,1,2,0:T(8,128)(2,1)} copy(bf16[16,1024,1,128]{3,1,2,0:T(8,128)(2,1)} %param.23) | data formatting | bytes 8388608
  5.4 0.0 copy-start
  5.4 0.0 copy-start.12
  5.5 0.0 copy-start.6
  5.5 0.0 copy-start.7
  5.5 0.0 copy-start.10
  5.5 2.0 %copy.102 = bf16[16,1024,1,128]{3,1,2,0:T(8,128)(2,1)} copy(bf16[16,1024,1,128]{3,1,2,0:T(8,128)(2,1)S(1)} %copy-done.1) | data formatting | bytes 8388608
  7.6 0.1 compare_and_fusion
  7.7 0.2 convert_reduce_fusion
  7.9 0.4 fusion.9
  8.3 0.1 le.40
  8.4 0.1 fusion.37
  8.5 0.1 reshape.321
  8.6 0.1 broadcast_minimum_fusion
  8.7 0.1 broadcast_in_dim.23
  8.8 0.1 le.36
  9.0 0.3 stack.26
  9.3 0.0 copy-start.3
  9.4 0.1 add_select_fusion
  9.5 0.7 convert_element_type.80.vecs
  10.2 0.3 fusion.12
  10.5 0.4 fusion.21
  11.0 0.4 fusion.20
  11.4 8.2 %fusion.2 = f32[64,1536]{1,0:T(8,128)S(1)} fusion(bf16[64,6144]{1,0:T(8,128)(2,1)S(1)} %bitcast.50, bf16[6144,1536]{1,0:T(8,128)(2,1)} %param.24, f32[1536]{0:T(1024)S(1)} %convert_element_type.67), kind=kOutput, calls=%fused_computation.7 | convolution fusion | flops 1208254464 | bytes 20060160 | tf_op jit(solution)/shard_map/dot_general | solution.py:43
  19.6 0.2 subtract_convert_fusion.1
  19.8 0.1 maximum_bitcast_fusion.1
  19.9 0.1 reshape.315
  19.9 0.2 subtract_convert_fusion
  20.2 0.2 maximum_bitcast_fusion
  20.4 0.1 copy.69
  20.4 0.2 fusion.57
  20.6 3.8 %fusion = (f32[16,48]{1,0:T(8,128)S(1)}, f32[16,48,1024]{2,1,0:T(8,128)S(1)}) fusion(s32[16,48]{1,0:T(8,128)S(1)} %le.36, s32[16,1024]{1,0:T(8,128)S(1)} %add_select_fusion, bf16[16,1024,1,128]{3,1,2,0:T(8,128)(2,1)} %copy.102, bf16[16,48,128]{2,0,1:T(8,128)(2,1)S(1)} %bitcast.55), kind=kOutput, calls=%fused_computation.4 | convolution fusion | flops 204471552 | bytes 7608320 | tf_op jit(solution)/shard_map/brd,bwd->brw/dot_general | solution.py:421
  24.5 8.1 %scatter_fusion = bf16[16,1024,128]{2,1,0:T(8,128)(2,1)} fusion(bf16[16,1024,128]{2,1,0:T(8,128)(2,1)} %bitcast.46, s32[64]{0:T(128)S(1)} %reshape.321, bf16[64,128]{1,0:T(8,128)(2,1)S(1)} %bitcast.63), kind=kCustom, calls=%fused_computation | custom fusion | bytes 49664 | tf_op jit(solution)/shard_map/scatter | solution.py:442
  32.6 0.1 fusion.27
  32.7 1.0 fusion.5
  33.8 0.1 copy.78
  33.8 0.1 copy.76
  33.9 0.1 copy.77
  34.1 0.1 copy.79
  34.2 2.9 %fusion.7 = f32[16,48,128]{2,1,0:T(8,128)S(1)} fusion(f32[16,48,1024]{2,1,0:T(8,128)S(1)} %get-tuple-element.10, f32[16,48]{1,0:T(8,128)S(1)} %max.17, s32[16,48]{1,0:T(8,128)S(1)} %le.36, s32[16,1024]{1,0:T(8,128)S(1)} %add_select_fusion, bf16[16,1024,1,128]{3,1,2,0:T(8,128)(2,1)} %copy.103), kind=kOutput, calls=%fused_computation.14 | convolution fusion | flops 206045184 | bytes 7804928 | tf_op jit(solution)/shard_map/brw,bwd->brd/dot_general | solution.py:427
  37.1 0.4 convolution_add_fusion.1
  37.5 0.1 copy.74
  37.7 8.1 %scatter_fusion.1 = bf16[16,1024,128]{2,1,0:T(8,128)(2,1)} fusion(bf16[16,1024,128]{2,1,0:T(8,128)(2,1)} %bitcast.51, s32[64]{0:T(128)S(1)} %reshape.321, bf16[64,128]{1,0:T(8,128)(2,1)S(1)} %bitcast.62), kind=kCustom, calls=%fused_computation.1 | custom fusion | bytes 49664 | tf_op jit(solution)/shard_map/scatter | solution.py:443
  45.8 0.1 copy.75
  45.9 0.1 reshape.312
  46.0 0.9 select_maximum_fusion.part
  46.9 82.0 %shard_map.211 = bf16[4,16,6144]{2,1,0:T(8,128)(2,1)} custom-call(f32[4,32,896]{2,1,0:T(8,128)} %select_maximum_fusion.part, bf16[4,16,6144]{2,1,0:T(8,128)(2,1)} %x_hbm.1, f32[8,6144]{1,0:T(8,128)} %convert_element_type.80.vecs, bf16[1536,6144]{1,0:T(8,128)(2,1)} %wo.1, bf16[6144,6144]{1,0:T(8,128)(2,1)} %wfc.1, bf16[6144,6144]{1,0:T(8,128)(2,1)} %wproj.1), custom_call_target="tpu_custom_call" | custom-call | tf_op jit(solution)/shard_map/pallas_call | solution.py:375
  128.9 2.1 %copy.104 = bf16[4,16,6144]{2,1,0:T(8,128)(2,1)} copy(bf16[4,16,6144]{2,1,0:T(8,128)(2,1)} %shard_map.211) | data formatting | bytes 1572864
  (50 shorter events, 0.3 us)
Async XLA Ops:
  0.6 4.8 %copy-start.1 = (bf16[16,1024,1,128]{3,1,2,0:T(8,128)(2,1)S(1)}, bf16[16,1024,1,128]{3,1,2,0:T(8,128)(2,1)}, u32[]{:S(2)}) copy-start(bf16[16,1024,1,128]{3,1,2,0:T(8,128)(2,1)} %param.22) | copy-start | bytes 12582916
  5.4 2.1 %copy-start.11 = (s32[16]{0:T(128)S(1)}, s32[16]{0:T(128)}, u32[]{:S(2)}) copy-start(s32[16]{0:T(128)} %param.21) | copy-start | bytes 196
  5.4 2.1 %copy-start.13 = (bf16[128]{0:T(256)(128)(2,1)S(1)}, bf16[128]{0:T(256)(128)(2,1)}, u32[]{:S(2)}) copy-start(bf16[128]{0:T(256)(128)(2,1)} %param.27) | copy-start | bytes 772
  5.4 2.2 %copy-start.14 = (bf16[128]{0:T(256)(128)(2,1)S(1)}, bf16[128]{0:T(256)(128)(2,1)}, u32[]{:S(2)}) copy-start(bf16[128]{0:T(256)(128)(2,1)} %param.29) | copy-start | bytes 772
  5.4 2.3 %copy-start = (bf16[4,16,6144]{2,1,0:T(8,128)(2,1)S(1)}, bf16[4,16,6144]{2,1,0:T(8,128)(2,1)}, u32[]{:S(2)}) copy-start(bf16[4,16,6144]{2,1,0:T(8,128)(2,1)} %x_hbm.1) | copy-start | bytes 2359300
  5.4 3.2 %copy-start.12 = (bf16[1536]{0:T(1024)(128)(2,1)S(1)}, bf16[1536]{0:T(1024)(128)(2,1)}, u32[]{:S(2)}) copy-start(bf16[1536]{0:T(1024)(128)(2,1)} %param.25) | copy-start | bytes 9220
  5.4 3.4 %copy-start.4 = (bf16[6144]{0:T(1024)(128)(2,1)S(1)}, bf16[6144]{0:T(1024)(128)(2,1)}, u32[]{:S(2)}) copy-start(bf16[6144]{0:T(1024)(128)(2,1)} %param.31) | copy-start | bytes 36868
  5.4 3.4 %copy-start.5 = (bf16[6144]{0:T(1024)(128)(2,1)S(1)}, bf16[6144]{0:T(1024)(128)(2,1)}, u32[]{:S(2)}) copy-start(bf16[6144]{0:T(1024)(128)(2,1)} %param.32) | copy-start | bytes 36868
  5.5 3.4 %copy-start.6 = (bf16[6144]{0:T(1024)(128)(2,1)S(1)}, bf16[6144]{0:T(1024)(128)(2,1)}, u32[]{:S(2)}) copy-start(bf16[6144]{0:T(1024)(128)(2,1)} %param.33) | copy-start | bytes 36868
  5.5 3.4 %copy-start.7 = (bf16[6144]{0:T(1024)(128)(2,1)S(1)}, bf16[6144]{0:T(1024)(128)(2,1)}, u32[]{:S(2)}) copy-start(bf16[6144]{0:T(1024)(128)(2,1)} %param.34) | copy-start | bytes 36868
  5.5 3.5 %copy-start.8 = (bf16[6144]{0:T(1024)(128)(2,1)S(1)}, bf16[6144]{0:T(1024)(128)(2,1)}, u32[]{:S(2)}) copy-start(bf16[6144]{0:T(1024)(128)(2,1)} %param.35) | copy-start | bytes 36868
  5.5 3.5 %copy-start.9 = (bf16[6144]{0:T(1024)(128)(2,1)S(1)}, bf16[6144]{0:T(1024)(128)(2,1)}, u32[]{:S(2)}) copy-start(bf16[6144]{0:T(1024)(128)(2,1)} %param.37) | copy-start | bytes 36868
  5.5 3.5 %copy-start.10 = (bf16[6144]{0:T(1024)(128)(2,1)S(1)}, bf16[6144]{0:T(1024)(128)(2,1)}, u32[]{:S(2)}) copy-start(bf16[6144]{0:T(1024)(128)(2,1)} %param.39) | copy-start | bytes 36868
  7.5 3.0 %copy-start.2 = (bf16[6144,128]{1,0:T(8,128)(2,1)S(1)}, bf16[6144,128]{1,0:T(8,128)(2,1)}, u32[]{:S(2)}) copy-start(bf16[6144,128]{1,0:T(8,128)(2,1)} %param.28) | copy-start | bytes 4718596
  9.3 1.6 %copy-start.3 = (bf16[6144,128]{1,0:T(8,128)(2,1)S(1)}, bf16[6144,128]{1,0:T(8,128)(2,1)}, u32[]{:S(2)}) copy-start(bf16[6144,128]{1,0:T(8,128)(2,1)} %param.26) | copy-start | bytes 4718596
